TPU v7x, 256 devices: a 8x8x2 block of a 8x8x16 slice. The times are simulated.
256 devices in a mesh: parts: 2 (over z), seq: 128 (over x, y, core).
Axes of the slice: x: 8, y: 8, z: 2, core: 2. Of those that a mesh axis runs over, the one named last changes fastest.
The devices are a block of a 8x8x16 slice.
Arguments:
- token_ids: int32 [4, 4], P(None, 'parts'), parts along dimension 1, may hold values from 0 to 76031
- lengths: int32 [4], P('parts'), parts along dimension 0, may hold values from 24576 to 32768, as said below
- embed_table: bfloat16 [76032, 5120], P('seq'), may hold values from -6 to 6
- attn_gain: bfloat16 [5120], replicated, may hold values from 0.25 to 1.75
- w_qkv: bfloat16 [5120, 7168], P('seq'), may hold values from -0.3125 to 0.3125
- qkv_bias: float32 [7168], replicated, may hold values from -8 to 8
- cache_keys: bfloat16 [4, 32768, 1024], P('parts', 'seq'), parts along dimension 0, may hold values from -300 to 300
- cache_values: bfloat16 [4, 32768, 1024], P('parts', 'seq'), parts along dimension 0, may hold values from -6 to 6
- w_out: bfloat16 [5120, 5120], P(None, 'seq'), may hold values from -0.078125 to 0.078125
- mlp_gain: bfloat16 [5120], replicated, may hold values from 0.25 to 1.75
- w_gate: bfloat16 [5120, 16384], P(None, 'seq'), may hold values from -0.078125 to 0.078125
- w_up: bfloat16 [5120, 16384], P(None, 'seq'), may hold values from -0.078125 to 0.078125
- w_down: bfloat16 [16384, 5120], P('seq'), may hold values from -0.1875 to 0.1875
Outputs:
- attended: bfloat16 [4, 4, 5120], P(None, 'parts'), parts along dimension 1
- layer_out: bfloat16 [4, 4, 5120], P(None, 'parts', 'seq'), parts along dimension 1
There are 2 independent parts, one for each index of `parts`. A program takes and returns all parts, laid end to end along the dimension named above; an argument that names none is the same for every part. Nothing has to cross between parts.
Inputs may be any that keep to these rules, and one draw needn't show every extreme that they name: Cache positions lengths[b] and later are unused; the first prompt fills the whole cache of 32768 positions.
All inputs are finite; a program needn't handle non-finite values.
Results may differ from a plain program's by a relative error of at most 0.017.
The roundings to bfloat16 on the way count: a program that leaves them out, or rounds other values in their place, can miss the bound.
Values may be sent and summed in bfloat16 or wider, within the bound.
No kernel may reach another device: no remote copies, remote signals or barrier semaphores. Data moves between devices by JAX's collectives and lax.ppermute only.
A program may use at most 128 MiB of HBM per device.

v0:
```python
import math
import jax
import jax.numpy as jnp
from jax import lax
from jax.sharding import Mesh
from jax.sharding import PartitionSpec as P

HEADS = 40
KV_HEADS = 8
HEAD_DIM = 128
SEQ = ("seq_0", "seq_1", "seq_2")
NORM_EPS = 1e-06
ROPE_BASE = 1000000.0
MASKED = -1e30


def gathered_once(array, axis):
    leaves = jax.tree.leaves(array)
    order = sorted(range(len(leaves)), key=lambda k: -leaves[k].size)
    width = (1, *leaves[order[0]].shape)[-1]
    lines = [
        jnp.pad(leaves[k].reshape(-1), (0, -leaves[k].size % width)).reshape(-1, width)
        for k in order
    ]
    both, at, found = (lax.all_gather(jnp.concatenate(lines), axis), 0, {})
    for k, line in zip(order, lines):
        slab = both[:, at : at + len(line)].reshape(len(both), -1)
        found[k] = slab[:, : leaves[k].size].reshape(-1, *leaves[k].shape)
        at += len(line)
    numbers = iter(range(len(leaves)))
    return jax.tree.map(lambda _: found[next(numbers)], array)


def combined_by_axis(array, axes, combine):
    for axis in axes:
        pieces = gathered_once(array, axis)
        array = jax.tree.map(lambda part: part[0], pieces)
        for k in range(1, lax.axis_size(axis)):
            array = combine(array, jax.tree.map(lambda part: part[k], pieces))
    return array


def sum_in_order(parts, axes, order):
    dims = [lax.axis_size(a) for a in axes]
    parts = parts.reshape(*dims, *parts.shape[1:])
    parts = parts.transpose(*order, *range(len(axes), parts.ndim))
    parts = parts.reshape(-1, *parts.shape[len(axes) :])
    for k in order:
        parts = lax.psum_scatter(parts, axes[k], scatter_dimension=0, tiled=True)
    return parts[0]


def cut_along(array, dim, devices):
    before, after = (array.shape[:dim], array.shape[dim + 1 :])
    return jnp.moveaxis(array.reshape(*before, devices, -1, *after), dim, 0)


def scatter_axes(array, axes, order, dim):
    devices = lax.axis_size(axes)
    return sum_in_order(cut_along(array, dim, devices), axes, order)


def rms_normalize(rows, gain):
    mean_square = jnp.mean(rows * rows, axis=-1, keepdims=True)
    return (rows * lax.rsqrt(mean_square + NORM_EPS) * gain.astype(jnp.float32)).astype(
        jnp.bfloat16
    )


def rotate(vectors, positions):
    half_dim = vectors.shape[-1] // 2
    frequency = ROPE_BASE ** (-2.0 * jnp.arange(half_dim, dtype=jnp.float32) / vectors.shape[-1])
    angles = positions.astype(jnp.float32)[..., None, None] * frequency
    cosine = jnp.cos(angles)
    sine_part = jnp.sin(angles)
    widened = vectors.astype(jnp.float32)
    first_half = widened[..., :half_dim]
    second = widened[..., half_dim:]
    joined = jnp.concatenate(
        [first_half * cosine - second * sine_part, second * cosine + first_half * sine_part],
        axis=-1,
    )
    return joined.astype(jnp.bfloat16)


def combine_partials(earlier, latter):
    top_one, total_one, sum_one = earlier
    top_two, total_two, sum_two = latter
    joined_top = jnp.maximum(top_one, top_two)
    scale_one = jnp.exp(top_one - joined_top)
    scale_two = jnp.exp(top_two - joined_top)
    return (
        joined_top,
        total_one * scale_one + total_two * scale_two,
        sum_one * scale_one[..., None] + sum_two * scale_two[..., None],
    )


def body(
    token_ids,
    lengths,
    embed_table,
    attn_gain,
    w_qkv,
    qkv_bias,
    cache_keys,
    cache_values,
    w_out,
    mlp_gain,
    w_gate,
    w_up,
    w_down,
):
    rank = lax.axis_index(SEQ)
    step_count, batch_count = token_ids.shape
    model_width = embed_table.shape[1]
    vocab_rows = embed_table.shape[0]
    query_width = HEADS * HEAD_DIM
    key_width = KV_HEADS * HEAD_DIM
    group_size = HEADS // KV_HEADS
    local_ids = token_ids - rank * vocab_rows
    inside = (local_ids >= 0) & (local_ids < vocab_rows)
    picked = jnp.take(embed_table, jnp.clip(local_ids, 0, vocab_rows - 1), axis=0)
    partial_rows = jnp.where(inside[..., None], picked.astype(jnp.float32), 0.0)
    stream = lax.psum(partial_rows, SEQ)
    normed = rms_normalize(stream, attn_gain).reshape(-1, model_width)
    feature_rows = w_qkv.shape[0]
    normed_local = lax.dynamic_slice_in_dim(normed, rank * feature_rows, feature_rows, 1)
    joint_partial = jnp.dot(normed_local, w_qkv, preferred_element_type=jnp.float32)
    joint_summed = lax.psum(joint_partial, SEQ)
    joint = (joint_summed + qkv_bias).astype(jnp.bfloat16).reshape(step_count, batch_count, -1)
    query_part = joint[..., :query_width].reshape(step_count, batch_count, HEADS, HEAD_DIM)
    key_part = joint[..., query_width : query_width + key_width].reshape(
        step_count, batch_count, KV_HEADS, HEAD_DIM
    )
    value_part = joint[..., query_width + key_width :].reshape(
        step_count, batch_count, KV_HEADS, HEAD_DIM
    )
    positions = lengths[None, :] + jnp.arange(step_count, dtype=jnp.int32)[:, None]
    queries = rotate(query_part, positions)
    new_keys = rotate(key_part, positions)
    grouped = queries.reshape(step_count, batch_count, KV_HEADS, group_size, HEAD_DIM)
    score_scale = 1.0 / math.sqrt(HEAD_DIM)
    local_len = cache_keys.shape[1]
    key_blocks = cache_keys.reshape(batch_count, local_len, KV_HEADS, HEAD_DIM)
    value_blocks = cache_values.reshape(batch_count, local_len, KV_HEADS, HEAD_DIM)
    scores = (
        jnp.einsum("sbkgd,bpkd->bkgsp", grouped, key_blocks, preferred_element_type=jnp.float32)
        * score_scale
    )
    places = rank * local_len + jnp.arange(local_len, dtype=jnp.int32)
    valid = (places[None, :] < lengths[:, None])[:, None, None, None, :]
    masked = jnp.where(valid, scores, MASKED)
    local_top = jnp.max(masked, axis=-1)
    weights = jnp.where(valid, jnp.exp(masked - local_top[..., None]), 0.0)
    local_total = jnp.sum(weights, axis=-1)
    local_sum = jnp.einsum(
        "bkgsp,bpkd->bkgsd",
        weights.astype(jnp.bfloat16),
        value_blocks,
        preferred_element_type=jnp.float32,
    )
    merged_top, merged_total, merged_sum = combined_by_axis(
        (local_top, local_total, local_sum), SEQ, combine_partials
    )
    new_scores = (
        jnp.einsum("sbkgd,tbkd->bkgst", grouped, new_keys, preferred_element_type=jnp.float32)
        * score_scale
    )
    step_index = jnp.arange(step_count, dtype=jnp.int32)
    causal = step_index[:, None] >= step_index[None, :]
    new_masked = jnp.where(causal, new_scores, MASKED)
    final_top = jnp.maximum(merged_top, jnp.max(new_masked, axis=-1))
    rescale = jnp.exp(merged_top - final_top)
    new_weights = jnp.where(causal, jnp.exp(new_masked - final_top[..., None]), 0.0)
    final_total = merged_total * rescale + jnp.sum(new_weights, axis=-1)
    final_sum = merged_sum * rescale[..., None] + jnp.einsum(
        "bkgst,tbkd->bkgsd",
        new_weights.astype(jnp.bfloat16),
        value_part,
        preferred_element_type=jnp.float32,
    )
    attended = jnp.transpose(final_sum / final_total[..., None], (3, 0, 1, 2, 4))
    attended = attended.reshape(step_count, batch_count, query_width).astype(jnp.bfloat16)
    shard_cols = w_out.shape[1]
    projected = jnp.dot(
        attended.reshape(-1, query_width), w_out, preferred_element_type=jnp.float32
    )
    stream_shard = lax.dynamic_slice_in_dim(stream, rank * shard_cols, shard_cols, 2)
    mid_shard = stream_shard + projected.reshape(step_count, batch_count, shard_cols)
    mid_rows = lax.all_gather(mid_shard, SEQ, axis=2, tiled=True)
    normed_mid = rms_normalize(mid_rows, mlp_gain)
    flat_rows = normed_mid.reshape(-1, model_width)
    gate = jnp.dot(flat_rows, w_gate, preferred_element_type=jnp.float32)
    upper = jnp.dot(flat_rows, w_up, preferred_element_type=jnp.float32)
    hidden = (jax.nn.silu(gate) * upper).astype(jnp.bfloat16)
    down_terms = jnp.dot(hidden, w_down, preferred_element_type=jnp.float32).reshape(
        step_count, batch_count, model_width
    )
    summed = scatter_axes(down_terms, SEQ, (2, 1, 0), 2)
    layer_out = (mid_shard + summed).astype(jnp.bfloat16)
    return (attended, layer_out)


def solution(mesh):
    finer = Mesh(
        mesh.devices.reshape(mesh.shape["parts"], 8, 8, 2), ("parts", "seq_0", "seq_1", "seq_2")
    )
    return jax.shard_map(
        body,
        mesh=finer,
        in_specs=(
            P(None, "parts"),
            P("parts"),
            P(SEQ, None),
            P(),
            P(SEQ, None),
            P(),
            P("parts", SEQ, None),
            P("parts", SEQ, None),
            P(None, SEQ),
            P(),
            P(None, SEQ),
            P(None, SEQ),
            P(SEQ, None),
        ),
        out_specs=(P(None, "parts", None), P(None, "parts", SEQ)),
        check_vma=False,
    )
```

profile of v0, /device:TPU:528, one launch (start us, length us, event | category | flops | bytes accessed | tf_op | source)
XLA Modules:
  0.0 717.2 jit_solution(17745230185070453889)
XLA Ops:
  7.3 0.8 compare_and_fusion
  8.3 4.2 gather_fusion
  12.8 0.8 convert_select_fusion
  14.0 0.3 copy.256
  14.4 1.1 copy-done.3
  15.5 0.3 copy.257
  15.8 1.1 bitcast_bitcast_fusion
  16.9 195.6 %all-reduce.14.cloned.1.call-done = f32[4,2,5120]{2,1,0:T(2,128)} async-done(((f32[4,2,5120]{2,1,0:T(2,128)}), f32[4,2,5120]{2,1,0:T(2,128)}) %all-reduce.14.cloned.1.call-update) | async-done | bytes 163856 | tf_op jit(solution)/shard_map/psum | solution.py:125
  212.4 1.1 multiply_reduce_fusion.1
  213.5 1.1 multiply_convert_fusion.1
  214.6 1.0 fusion.77
  215.8 181.4 %all-reduce.16.cloned.1.call-done = f32[8,7168]{1,0:T(8,128)} async-done(((f32[8,7168]{1,0:T(8,128)}), f32[8,7168]{1,0:T(8,128)}) %all-reduce.16.cloned.1.call-update) | async-done | bytes 229392 | tf_op jit(solution)/shard_map/psum | solution.py:130
  397.2 1.0 add_convert_fusion
  398.3 0.3 subtract_convert_fusion
  398.6 0.5 fusion.92
  399.2 0.2 copy.205
  399.4 0.3 fusion.13
  400.1 1.5 fusion.9
  401.6 0.7 maximum_bitcast_fusion
  402.4 38.6 %all-gather.9.cloned.1.call-done = f32[8,326,128]{2,1,0:T(8,128)} async-done(((f32[1,326,128]{2,1,0:T(8,128)}), f32[8,326,128]{2,1,0:T(8,128)}) %all-gather.9.cloned.1.call-update) | async-done | bytes 1335312 | tf_op jit(solution)/shard_map/all_gather | solution.py:25
  441.0 0.8 fusion.88
  442.1 2.0 fusion.39
  444.1 0.7 maximum_bitcast_fusion.1
  445.1 0.8 fusion.93
  446.0 38.5 %all-gather.11.cloned.1.call-done = f32[8,326,128]{2,1,0:T(8,128)} async-done(((f32[1,326,128]{2,1,0:T(8,128)}), f32[8,326,128]{2,1,0:T(8,128)}) %all-gather.11.cloned.1.call-update) | async-done | bytes 1335312 | tf_op jit(solution)/shard_map/all_gather | solution.py:25
  484.5 0.8 fusion.87
  485.6 2.0 fusion.18
  487.6 2.1 all-gather.5
  491.8 0.5 fusion.4
  492.4 0.4 copy-done.10
  492.8 1.0 convolution_add_fusion.1
  493.9 56.9 %all_gather.27 = f32[4,2,5120]{0,1,2:T(2,128)} all-gather(f32[4,2,40]{0,1,2:T(2,128)S(1)} %copy.230), channel_id=1, replica_groups=mesh['parts'=2,'seq_0'=8,'seq_1'=8,'seq_2'=2] {'seq_0','seq_1','seq_2'}, dimensions={2}, use_global_device_ids=true | all-gather | bytes 165120 | tf_op jit(solution)/shard_map/all_gather | solution.py:191
  550.8 5.6 copy.233
  556.5 7.0 multiply_reduce_fusion
  564.0 0.3 fusion.94
  564.2 1.9 fusion.8
  566.1 0.4 reshape_reshape.2
  566.7 1.1 copy.236
  568.0 0.6 dynamic-slice
  569.3 30.1 %all-reduce.18.cloned.1.call-done = f32[128,4,2,40]{3,1,2,0:T(4,128)} async-done(((f32[128,4,2,40]{3,1,2,0:T(4,128)}), f32[128,4,2,40]{3,1,2,0:T(4,128)}) %all-reduce.18.cloned.1.call-update) | async-done | bytes 163856
  599.4 1.7 constant_dynamic-slice_fusion.2
  601.1 0.6 dynamic-slice.2
  601.7 0.6 dynamic-slice.4
  603.0 75.6 %all-reduce.20.cloned.1.call-done = f32[64,4,2,40]{3,1,2,0:T(4,128)} async-done(((f32[64,4,2,40]{3,1,2,0:T(4,128)}), f32[64,4,2,40]{3,1,2,0:T(4,128)}) %all-reduce.20.cloned.1.call-update) | async-done | bytes 81936
  678.7 0.8 constant_dynamic-slice_fusion.1
  679.4 29.7 %all-reduce.8 = f32[8,4,2,40]{3,1,2,0:T(4,128)S(1)} all-reduce(f32[8,4,2,40]{3,1,2,0:T(4,128)S(1)} %constant_dynamic-slice_fusion.1), channel_id=7, replica_groups=mesh['parts'=2,'seq_0'=8,'seq_1'=8,'seq_2'=2] {'seq_0'}, use_global_device_ids=true, to_apply=%region_10.11.clone | all-reduce | flops 2560 | bytes 20480
  709.1 0.6 constant_dynamic-slice_fusion
  709.7 0.6 fusion.70
  (121 shorter events, 5.7 us)
Async XLA Ops:
  7.2 557.1 %copy-start = (bf16[128,5120]{1,0:T(8,128)(2,1)S(1)}, bf16[128,5120]{1,0:T(8,128)(2,1)}, u32[]{:S(2)}) copy-start(bf16[128,5120]{1,0:T(8,128)(2,1)} %param.25) | copy-start | bytes 3932164
  7.2 6.6 copy-start.7
  7.2 6.6 copy-start.9
  7.2 6.8 copy-start.2
  7.2 205.2 %all-reduce.14.cloned.1.call-start = ((), (), s32[]{:S(2)}) async-start(), calls=%async_computation | async-start | bytes 327680 | tf_op jit(solution)/shard_map/psum | solution.py:125
  13.7 383.5 %all-reduce.16.cloned.1.call-start = ((), (), s32[]{:S(2)}) async-start(), calls=%async_computation.1 | async-start | bytes 458752 | tf_op jit(solution)/shard_map/psum | solution.py:130
  14.3 1.2 copy-start.3
  15.8 198.8 %copy-start.4 = (bf16[40,7168]{1,0:T(8,128)(2,1)S(1)}, bf16[40,7168]{1,0:T(8,128)(2,1)}, u32[]{:S(2)}) copy-start(bf16[40,7168]{1,0:T(8,128)(2,1)} %param.17) | copy-start | bytes 1720324
  16.9 380.3 %copy-start.6 = (f32[7168]{0:T(1024)S(1)}, f32[7168]{0:T(1024)}, u32[]{:S(2)}) copy-start(f32[7168]{0:T(1024)} %param.18) | copy-start | bytes 86020
  215.7 225.3 %all-gather.9.cloned.1.call-start = ((), (), s32[]{:S(2)}) async-start(), calls=%async_computation.2 | async-start | bytes 1511424 | tf_op jit(solution)/shard_map/all_gather | solution.py:25
  402.3 42.6 %copy-start.8 = (bf16[5120]{0:T(1024)(128)(2,1)S(1)}, bf16[5120]{0:T(1024)(128)(2,1)}, u32[]{:S(2)}) copy-start(bf16[5120]{0:T(1024)(128)(2,1)} %param.22) | copy-start | bytes 30724
  402.3 82.2 %all-gather.11.cloned.1.call-start = ((), (), s32[]{:S(2)}) async-start(), calls=%async_computation.3 | async-start | bytes 1511424 | tf_op jit(solution)/shard_map/all_gather | solution.py:25
  444.8 154.6 %all-reduce.18.cloned.1.call-start = ((), (), s32[]{:S(2)}) async-start(), calls=%async_computation.4 | async-start | bytes 1048576
  491.8 1.0 copy-start.10
  492.8 58.0 %copy-start.5 = (bf16[4,2,5120]{2,1,0:T(2,128)(2,1)}, bf16[4,2,5120]{2,1,0:T(2,128)(2,1)S(1)}, u32[]{:S(2)}) copy-start(bf16[4,2,5120]{2,1,0:T(2,128)(2,1)S(1)} %convert_element_type.84) | copy-start | bytes 245764
  556.5 7.5 %copy-start.1 = (bf16[5120,128]{1,0:T(8,128)(2,1)S(1)}, bf16[5120,128]{1,0:T(8,128)(2,1)}, u32[]{:S(2)}) copy-start(bf16[5120,128]{1,0:T(8,128)(2,1)} %param.23) | copy-start | bytes 3932164
  566.5 1.5 copy-start.13
  566.7 34.4 %copy-start.12 = (u32[256]{0:T(256)S(1)}, u32[256]{0:T(256)}, u32[]{:S(2)}) copy-start(u32[256]{0:T(256)} %constant.90) | copy-start | bytes 3076
  566.7 35.0 %copy-start.11 = (u32[256]{0:T(256)S(1)}, u32[256]{0:T(256)}, u32[]{:S(2)}) copy-start(u32[256]{0:T(256)} %constant.94) | copy-start | bytes 3076
  567.9 110.7 %all-reduce.20.cloned.1.call-start = ((), (), s32[]{:S(2)}) async-start(), calls=%async_computation.5 | async-start | bytes 524288
Sparse Core Ops, SparseCore 0:
  13.8 198.6 all-reduce.13
  215.8 181.3 all-reduce.15
  402.5 38.5 all-gather.8
  444.9 39.5 all-gather.10
  568.1 31.3 all-reduce.17
  601.6 77.0 all-reduce.19
where the time goes:
time: 718 us; the launch traced here: 717 us
  waiting for transfers between devices  560 us (78%)
  blocking collectives  88.7 us (12%)
  local copies, waits for them, and re-layouts  25.4 us (4%)
  other arithmetic  19.2 us (3%)
  between operations  16 us (2%)
  matrix products  7.37 us (1%)
    psum x1, waiting for transfers between devices, body(): stream = lax.psum(partial_rows, SEQ)  196 us
    psum x1, waiting for transfers between devices, body(): joint_summed = lax.psum(joint_partial, SEQ)  181 us
    unnamed x8, waiting for transfers between devices  106 us
    all_gather x2, waiting for transfers between devices, gathered_once(): both, at, found = (lax.all_gather(jnp.concatenate(lines), axis), 0, {})  77.1 us
    all_gather x1, blocking collectives, body(): mid_rows = lax.all_gather(mid_shard, SEQ, axis=2, tiled=True)  56.9 us
    unnamed x1, blocking collectives  29.7 us
  transfers between devices with their start and end apart: 6, of which 6 were waited for; matrix products, arithmetic and copies ran while one was open for 1% of the time, Pallas kernels for 0%

commit v1 on v0

--- a/solution.py
+++ b/solution.py
@@ -188,7 +188,9 @@
     )
     stream_shard = lax.dynamic_slice_in_dim(stream, rank * shard_cols, shard_cols, 2)
     mid_shard = stream_shard + projected.reshape(step_count, batch_count, shard_cols)
-    mid_rows = lax.all_gather(mid_shard, SEQ, axis=2, tiled=True)
+    mid_rows = jnp.concatenate(
+        lax.all_to_all(jnp.stack([mid_shard] * lax.axis_size(SEQ)), SEQ, 0, 0), axis=2
+    )
     normed_mid = rms_normalize(mid_rows, mlp_gain)
     flat_rows = normed_mid.reshape(-1, model_width)
     gate = jnp.dot(flat_rows, w_gate, preferred_element_type=jnp.float32)

time: 718 us -> 673 us (0.937)
  blocking collectives: 88.7 us -> 31.8 us
  starting transfers between devices: 0.38 us -> 13.3 us
    all_gather x1 -> x0, blocking collectives: 56.9 us -> none  [body(): mid_rows = lax.all_gather(mid_shard, SEQ, axis=2, tiled=True)]
    all_to_all x0 -> x1, starting transfers between devices: none -> 13 us  [body(): lax.all_to_all(jnp.stack([mid_shard] * lax.axis_size(SEQ)), SEQ, 0, 0)]
    all_to_all x0 -> x1, waiting for transfers between devices: none -> 12.1 us  [body(): lax.all_to_all(jnp.stack([mid_shard] * lax.axis_size(SEQ)), SEQ, 0, 0)]
  transfers between devices with their start and end apart: 6 -> 7, of which waited for: 6 -> 7; matrix products, arithmetic and copies ran while one was open for 1% -> 1% of each run, Pallas kernels for 0% -> 0%
where the time goes in v1:
time: 673 us; the launch traced here: 672 us
  waiting for transfers between devices  567 us (84%)
  blocking collectives  31.8 us (5%)
  local copies, waits for them, and re-layouts  22.6 us (3%)
  between operations  16.1 us (2%)
  other arithmetic  14.3 us (2%)
  starting transfers between devices  13.3 us (2%)
  matrix products  6.87 us (1%)
    psum x1, waiting for transfers between devices, body(): stream = lax.psum(partial_rows, SEQ)  196 us
    psum x1, waiting for transfers between devices, body(): joint_summed = lax.psum(joint_partial, SEQ)  181 us
    unnamed x8, waiting for transfers between devices  101 us
    all_gather x2, waiting for transfers between devices, gathered_once(): both, at, found = (lax.all_gather(jnp.concatenate(lines), axis), 0, {})  77.2 us
    unnamed x1, blocking collectives  29.7 us
  transfers between devices with their start and end apart: 7, of which 7 were waited for; matrix products, arithmetic and copies ran while one was open for 1% of the time, Pallas kernels for 0%

profile of v1, /device:TPU:528, one launch (start us, length us, event | category | flops | bytes accessed | tf_op | source)
XLA Modules:
  0.0 672.0 jit_solution(771254569476138488)
XLA Ops:
  7.3 0.8 compare_and_fusion
  8.3 4.2 gather_fusion
  12.6 0.8 convert_select_fusion
  14.1 1.1 copy-done.3
  15.5 1.0 bitcast_bitcast_fusion
  16.6 195.6 %all-reduce.14.cloned.1.call-done = f32[4,2,5120]{2,0,1:T(4,128)} async-done(((f32[4,2,5120]{2,0,1:T(4,128)}), f32[4,2,5120]{2,0,1:T(4,128)}) %all-reduce.14.cloned.1.call-update) | async-done | bytes 163856 | tf_op jit(solution)/shard_map/psum | solution.py:125
  212.2 1.0 multiply_reduce_fusion.1
  213.3 1.0 multiply_convert_fusion.1
  214.4 1.0 fusion.79
  215.6 181.4 %all-reduce.16.cloned.1.call-done = f32[8,7168]{1,0:T(8,128)} async-done(((f32[8,7168]{1,0:T(8,128)}), f32[8,7168]{1,0:T(8,128)}) %all-reduce.16.cloned.1.call-update) | async-done | bytes 229392 | tf_op jit(solution)/shard_map/psum | solution.py:130
  397.0 1.0 add_convert_fusion
  398.4 0.5 fusion.95
  399.2 0.3 fusion.13
  399.9 1.5 fusion.9
  401.4 0.7 maximum_bitcast_fusion
  402.2 38.6 %all-gather.9.cloned.1.call-done = f32[8,326,128]{2,1,0:T(8,128)} async-done(((f32[1,326,128]{2,1,0:T(8,128)}), f32[8,326,128]{2,1,0:T(8,128)}) %all-gather.9.cloned.1.call-update) | async-done | bytes 1335312 | tf_op jit(solution)/shard_map/all_gather | solution.py:25
  440.8 0.8 fusion.91
  441.8 2.0 fusion.40
  443.8 0.7 maximum_bitcast_fusion.1
  444.8 0.8 fusion.96
  445.7 38.6 %all-gather.11.cloned.1.call-done = f32[8,326,128]{2,1,0:T(8,128)} async-done(((f32[1,326,128]{2,1,0:T(8,128)}), f32[8,326,128]{2,1,0:T(8,128)}) %all-gather.11.cloned.1.call-update) | async-done | bytes 1335312 | tf_op jit(solution)/shard_map/all_gather | solution.py:25
  484.3 0.8 fusion.90
  485.3 2.0 fusion.19
  487.3 2.1 all-gather.5
  491.5 0.5 fusion.4
  492.2 0.4 copy-done.10
  492.8 0.8 copy_add_fusion
  493.8 1.6 reshape.1156
  495.3 13.0 %all-to-all-start = ((f32[128,1,320]{2,1,0:T(1,128)}), f32[128,1,320]{2,1,0:T(1,128)S(1)}, u32[]{:S(2)}, u32[]{:S(2)}) async-start(f32[128,1,320]{2,1,0:T(1,128)} %reshape.1156), calls=%async_computation | async-start | bytes 393216 | tf_op jit(solution)/shard_map/all_to_all | solution.py:192
  508.4 12.1 %all-to-all-done = f32[128,1,320]{2,1,0:T(1,128)S(1)} async-done(((f32[128,1,320]{2,1,0:T(1,128)}), f32[128,1,320]{2,1,0:T(1,128)S(1)}, u32[]{:S(2)}, u32[]{:S(2)}) %all-to-all-start) | async-done | bytes 163872 | tf_op jit(solution)/shard_map/all_to_all | solution.py:192
  520.5 0.5 broadcast.229
  521.0 1.1 reduce.73
  522.1 0.8 reshape.1157
  522.9 0.4 multiply_reduce_fusion
  523.8 1.7 fusion.86
  525.6 0.6 fusion.8
  526.2 0.4 reshape_reshape.2
  526.8 1.1 copy.206
  528.1 0.6 dynamic-slice
  529.3 24.9 %all-reduce.18.cloned.1.call-done = f32[128,4,2,40]{3,1,2,0:T(4,128)} async-done(((f32[128,4,2,40]{3,1,2,0:T(4,128)}), f32[128,4,2,40]{3,1,2,0:T(4,128)}) %all-reduce.18.cloned.1.call-update) | async-done | bytes 163856
  554.3 1.7 constant_dynamic-slice_fusion.1
  556.0 0.7 dynamic-slice.4
  556.7 0.6 dynamic-slice.2
  557.9 75.6 %all-reduce.20.cloned.1.call-done = f32[64,4,2,40]{3,1,2,0:T(4,128)} async-done(((f32[64,4,2,40]{3,1,2,0:T(4,128)}), f32[64,4,2,40]{3,1,2,0:T(4,128)}) %all-reduce.20.cloned.1.call-update) | async-done | bytes 81936
  633.5 0.8 constant_dynamic-slice_fusion
  634.2 29.7 %all-reduce.8 = f32[8,4,2,40]{3,1,2,0:T(4,128)S(1)} all-reduce(f32[8,4,2,40]{3,1,2,0:T(4,128)S(1)} %constant_dynamic-slice_fusion), channel_id=7, replica_groups=mesh['parts'=2,'seq_0'=8,'seq_1'=8,'seq_2'=2] {'seq_0'}, use_global_device_ids=true, to_apply=%region_10.11.clone | all-reduce | flops 2560 | bytes 20480
  663.9 0.7 fusion.72
  664.6 0.6 copy.207
  (124 shorter events, 6.9 us)
Async XLA Ops:
  7.2 518.4 %copy-start = (bf16[128,5120]{1,0:T(8,128)(2,1)S(1)}, bf16[128,5120]{1,0:T(8,128)(2,1)}, u32[]{:S(2)}) copy-start(bf16[128,5120]{1,0:T(8,128)(2,1)} %param.25) | copy-start | bytes 3932164
  7.2 6.3 copy-start.9
  7.2 6.5 copy-start.7
  7.2 6.5 copy-start.2
  7.2 205.0 %all-reduce.14.cloned.1.call-start = ((), (), s32[]{:S(2)}) async-start(), calls=%async_computation.1 | async-start | bytes 327680 | tf_op jit(solution)/shard_map/psum | solution.py:125
  13.4 383.6 %all-reduce.16.cloned.1.call-start = ((), (), s32[]{:S(2)}) async-start(), calls=%async_computation.2 | async-start | bytes 458752 | tf_op jit(solution)/shard_map/psum | solution.py:130
  14.0 1.2 copy-start.3
  15.5 198.9 %copy-start.4 = (bf16[40,7168]{1,0:T(8,128)(2,1)S(1)}, bf16[40,7168]{1,0:T(8,128)(2,1)}, u32[]{:S(2)}) copy-start(bf16[40,7168]{1,0:T(8,128)(2,1)} %param.17) | copy-start | bytes 1720324
  16.6 380.4 %copy-start.6 = (f32[7168]{0:T(1024)S(1)}, f32[7168]{0:T(1024)}, u32[]{:S(2)}) copy-start(f32[7168]{0:T(1024)} %param.18) | copy-start | bytes 86020
  215.4 225.3 %all-gather.9.cloned.1.call-start = ((), (), s32[]{:S(2)}) async-start(), calls=%async_computation.3 | async-start | bytes 1511424 | tf_op jit(solution)/shard_map/all_gather | solution.py:25
  402.1 82.1 %all-gather.11.cloned.1.call-start = ((), (), s32[]{:S(2)}) async-start(), calls=%async_computation.4 | async-start | bytes 1511424 | tf_op jit(solution)/shard_map/all_gather | solution.py:25
  491.5 1.0 copy-start.10
  492.1 16.3 %copy-start.8 = (bf16[5120]{0:T(1024)(128)(2,1)S(1)}, bf16[5120]{0:T(1024)(128)(2,1)}, u32[]{:S(2)}) copy-start(bf16[5120]{0:T(1024)(128)(2,1)} %param.22) | copy-start | bytes 30724
  492.5 29.5 %copy-start.5 = (bf16[4,2,5120]{2,1,0:T(2,128)(2,1)}, bf16[4,2,5120]{2,1,0:T(2,128)(2,1)S(1)}, u32[]{:S(2)}) copy-start(bf16[4,2,5120]{2,1,0:T(2,128)(2,1)S(1)} %convert_element_type.85) | copy-start | bytes 245764
  495.3 25.1 %all-to-all-start = ((f32[128,1,320]{2,1,0:T(1,128)}), f32[128,1,320]{2,1,0:T(1,128)S(1)}, u32[]{:S(2)}, u32[]{:S(2)}) async-start(f32[128,1,320]{2,1,0:T(1,128)} %reshape.1156), calls=%async_computation | async-start | bytes 393216 | tf_op jit(solution)/shard_map/all_to_all | solution.py:192
  508.3 46.0 %all-reduce.18.cloned.1.call-start = ((), (), s32[]{:S(2)}) async-start(), calls=%async_computation.5 | async-start | bytes 1048576
  523.8 1.8 copy-start.1
  526.6 1.5 copy-start.13
  526.8 29.2 %copy-start.12 = (u32[256]{0:T(256)S(1)}, u32[256]{0:T(256)}, u32[]{:S(2)}) copy-start(u32[256]{0:T(256)} %constant.94) | copy-start | bytes 3076
  526.8 29.8 %copy-start.11 = (u32[256]{0:T(256)S(1)}, u32[256]{0:T(256)}, u32[]{:S(2)}) copy-start(u32[256]{0:T(256)} %constant.90) | copy-start | bytes 3076
  528.0 105.4 %all-reduce.20.cloned.1.call-start = ((), (), s32[]{:S(2)}) async-start(), calls=%async_computation.6 | async-start | bytes 524288
Sparse Core Ops, SparseCore 0:
  13.5 198.6 all-reduce.13
  215.6 181.3 all-reduce.15
  402.2 38.5 all-gather.8
  444.7 39.5 all-gather.10
  528.1 26.0 all-reduce.17
  556.4 76.9 all-reduce.19
